TPU v7x, 32 devices: a whole 2x2x4 slice. The times are simulated.
32 devices in a mesh: dp: 4 (over z), fsdp: 8 (over y, x, core).
Axes of the slice: x: 2, y: 2, z: 4, core: 2. Of those that a mesh axis runs over, the one named last changes fastest.
Arguments:
- hidden: bfloat16 [8192, 4096], P(('dp', 'fsdp')), may hold values from -6 to 6
- queries: bfloat16 [8192, 2048], P(('dp', 'fsdp')), may hold values from -6 to 6
- keys: bfloat16 [8192, 512], P(('dp', 'fsdp')), may hold values from -6 to 6
- target: bfloat16 [8192, 2048], P(('dp', 'fsdp')), may hold values from -6 to 6
- lengths: int32 [32], P(('dp', 'fsdp')), may hold values from 64 to 256
- value_weight_frozen: bfloat16 [4096, 512], P('fsdp'), may hold values from -0.09375 to 0.09375
- adapter_down_map: float32 [4096, 64], P('fsdp'), may hold values from -0.09375 to 0.09375
- adapter_up_map: float32 [64, 512], replicated, may hold values from -0.75 to 0.75
- average_down_map: float32 [4096, 64], P('fsdp'), may hold values from -0.09375 to 0.09375
- average_up_map: float32 [64, 512], replicated, may hold values from -0.75 to 0.75
Outputs:
- down_map_gradient: float32 [4096, 64], P('fsdp')
- up_map_gradient: float32 [64, 512], replicated
- average_down_next: float32 [4096, 64], P('fsdp')
- average_up_next: float32 [64, 512], replicated
- loss: float32 [], replicated
Inputs may be any that keep to these rules, and one draw needn't show every extreme that they name: `lengths`: slots at or past a sequence's length are padding.
All inputs are finite; a program needn't handle non-finite values.
Results may differ from a plain program's by a relative error of at most 0.0049.
Values may be sent and summed in bfloat16 or wider, within the bound.
A program may use at most 64 MiB of HBM per device.

v0:
```python
import math
import jax
import jax.numpy as jnp
from jax import lax
from jax.sharding import PartitionSpec as P

HEADS = 16
KEY_VALUE_HEADS = 4
HEAD_DIM = 128
adapter_scale = 2.0
average_decay = 0.9
learning_rate = 1.0
masked_score = -1e30


def per_device(
    hidden,
    queries,
    keys,
    target,
    lengths,
    value_weight_frozen,
    adapter_down_map,
    adapter_up_map,
    average_down_map,
    average_up_map,
):
    tok_rows = hidden.shape[0]
    group_size = HEADS // KEY_VALUE_HEADS
    seq_length = lengths[0]
    down_factor_slice = adapter_down_map.astype(jnp.bfloat16)
    up_factor_slice = adapter_up_map.astype(jnp.bfloat16)
    columns = hidden
    frozen_value_output = jnp.dot(
        columns,
        lax.all_gather(value_weight_frozen, "fsdp", axis=0, tiled=True),
        preferred_element_type=jnp.float32,
    )
    adapter_hidden = jnp.dot(
        columns,
        lax.all_gather(down_factor_slice, "fsdp", axis=0, tiled=True),
        preferred_element_type=jnp.float32,
    )
    adapter_hidden = adapter_hidden.astype(jnp.bfloat16)
    value_outputs = (
        frozen_value_output
        + adapter_scale
        * jnp.dot(adapter_hidden, up_factor_slice, preferred_element_type=jnp.float32)
    ).astype(jnp.bfloat16)
    position = jnp.arange(tok_rows, dtype=jnp.int32)
    allowed = (position[None, :] <= position[:, None]) & (position[None, :] < seq_length)
    q_heads = queries.reshape(tok_rows, KEY_VALUE_HEADS, group_size, HEAD_DIM)
    k_heads = keys.reshape(tok_rows, KEY_VALUE_HEADS, HEAD_DIM)
    v_heads = value_outputs.reshape(tok_rows, KEY_VALUE_HEADS, HEAD_DIM)
    scores = jnp.einsum(
        "tkgd,skd->kgts", q_heads, k_heads, preferred_element_type=jnp.float32
    ) / math.sqrt(HEAD_DIM)
    scores = jnp.where(allowed, scores, masked_score)
    row_max = jnp.max(scores, axis=-1, keepdims=True)
    weights = jnp.exp(scores - row_max)
    attn_probs = (weights / jnp.sum(weights, axis=-1, keepdims=True)).astype(jnp.bfloat16)
    output = jnp.einsum(
        "kgts,skd->tkgd", attn_probs, v_heads, preferred_element_type=jnp.float32
    ).reshape(tok_rows, HEADS * HEAD_DIM)
    live_rows = (position < seq_length)[:, None]
    differ = jnp.where(live_rows, output - target.astype(jnp.float32), 0.0)
    loss_local = jnp.sum(differ * differ)
    cotangent = differ.astype(jnp.bfloat16).reshape(tok_rows, KEY_VALUE_HEADS, group_size, HEAD_DIM)
    value_grad = jnp.einsum(
        "kgts,tkgd->skd", attn_probs, cotangent, preferred_element_type=jnp.float32
    )
    value_grad = value_grad.reshape(tok_rows, KEY_VALUE_HEADS * HEAD_DIM).astype(jnp.bfloat16)
    latent_grad = lax.dot_general(
        value_grad, up_factor_slice, (((1,), (1,)), ((), ())), preferred_element_type=jnp.float32
    ).astype(jnp.bfloat16)
    up_term = lax.dot_general(
        adapter_hidden, value_grad, (((0,), (0,)), ((), ())), preferred_element_type=jnp.float32
    )
    count_local = seq_length.astype(jnp.float32)
    columns = hidden
    down_map_gradient = lax.psum(
        adapter_scale
        * lax.dot_general(
            columns, latent_grad, (((0,), (0,)), ((), ())), preferred_element_type=jnp.float32
        ),
        "dp",
    )
    down_map_gradient = lax.psum_scatter(down_map_gradient, "fsdp", scatter_dimension=0, tiled=True)
    up_map_gradient, loss_sum, token_grand_count = lax.psum(
        (adapter_scale * up_term, loss_local, count_local), ("dp", "fsdp")
    )
    up_map_gradient = up_map_gradient / token_grand_count
    down_map_gradient = down_map_gradient / token_grand_count
    loss = loss_sum / (2.0 * token_grand_count)
    average_down_next = average_decay * average_down_map + (1.0 - average_decay) * (
        adapter_down_map - learning_rate * down_map_gradient
    )
    average_up_next = average_decay * average_up_map + (1.0 - average_decay) * (
        adapter_up_map - learning_rate * up_map_gradient
    )
    return (down_map_gradient, up_map_gradient, average_down_next, average_up_next, loss)


def solution(mesh):
    placed = (
        P(("dp", "fsdp"), None),
        P(("dp", "fsdp"), None),
        P(("dp", "fsdp"), None),
        P(("dp", "fsdp"), None),
        P(("dp", "fsdp")),
        P("fsdp", None),
        P("fsdp", None),
        P(),
        P("fsdp", None),
        P(),
    )
    return jax.shard_map(
        per_device,
        mesh=mesh,
        in_specs=placed,
        out_specs=(P("fsdp", None), P(), P("fsdp", None), P(), P()),
        check_vma=False,
    )
```

profile of v0, /device:TPU:0, one launch (start us, length us, event | category | flops | bytes accessed | tf_op | source)
XLA Modules:
  0.0 281.5 jit_solution(8382225691264275477)
XLA Ops:
  7.2 0.7 all-gather.2.cloned.1.call-update
  8.6 1.8 reshape.40
  10.4 1.0 reshape.39
  11.5 11.3 %all_gather.7 = bf16[4096,64]{0,1:T(8,128)(2,1)S(1)} all-gather(bf16[512,64]{0,1:T(8,128)(2,1)S(1)} %convert_element_type.36), channel_id=1, replica_groups=mesh['dp'=4,'fsdp'=8] {'fsdp'}, dimensions={0}, use_global_device_ids=true | all-gather | bytes 589824 | tf_op jit(solution)/shard_map/all_gather | solution.py:41
  22.9 1.4 convolution_convert_fusion.1
  24.3 0.7 fusion.10
  25.0 1.2 fusion.19
  26.3 1.8 divide_convert_fusion
  28.0 21.2 %all-gather.2.cloned.1.call-done = bf16[4096,512]{1,0:T(8,128)(2,1)} async-done(((bf16[512,512]{1,0:T(8,128)(2,1)}), bf16[4096,512]{1,0:T(8,128)(2,1)}) %all-gather.2.cloned.1.call-update) | async-done | bytes 4194320 | tf_op jit(solution)/shard_map/all_gather | solution.py:36
  49.2 3.4 %fusion.20 = f32[256,512]{1,0:T(8,128)S(1)} fusion(bf16[256,4096]{1,0:T(8,128)(2,1)S(1)} %copy-done, bf16[4096,512]{1,0:T(8,128)(2,1)} %all-gather.2.cloned.1.call-done), kind=kOutput, calls=%fused_computation.36 | convolution fusion | flops 1073741824 | bytes 6815744 | tf_op jit(solution)/shard_map/dot_general | solution.py:34
  52.7 0.3 fusion.8
  52.9 0.1 copy.27
  53.1 3.3 %fusion.21 = f32[4,128,4,256]{3,1,2,0:T(8,128)} fusion(bf16[256,4,128,1]{0,2,3,1:T(8,128)(2,1)S(1)} %bitcast.51, bf16[4,4,256,256]{2,3,1,0:T(8,128)(2,1)} %divide_convert_fusion), kind=kOutput, calls=%fused_computation.37 | convolution fusion | flops 268435456 | bytes 4456448 | tf_op jit(solution)/shard_map/kgts,skd->tkgd/dot_general | solution.py:62
  56.4 3.0 %copy.19 = f32[256,2048]{1,0:T(8,128)} copy(f32[256,2048]{0,1:T(8,128)} %bitcast.47) | data formatting | bytes 4194304 | tf_op jit(solution)/shard_map/reshape | solution.py:64
  59.5 3.6 %multiply_reduce_fusion = (f32[]{:T(128)}, bf16[256,2048]{1,0:T(8,128)(2,1)}) fusion(f32[256,2048]{1,0:T(8,128)} %copy.19, bf16[256,2048]{1,0:T(8,128)(2,1)S(1)} %copy-done.2, pred[256]{0:T(512)(128)(4,1)S(1)} %iota_compare_fusion.1), kind=kLoop, calls=%fused_computation.7 | loop fusion | flops 3145727 | bytes 4194564 | tf_op jit(solution)/shard_map/reduce_sum | solution.py:67
  63.1 1.5 copy.30
  64.6 2.4 fusion.9
  67.0 1.8 fusion.1
  69.0 0.9 convolution_multiply_fusion.2
  69.9 39.5 %all-reduce = (f32[]{:T(128)}, f32[]{:T(128)}) all-reduce(f32[]{:T(128)S(6)} %convert_element_type.47, f32[]{:T(128)} %get-tuple-element.11), channel_id=1, replica_groups=mesh['dp'=4,'fsdp'=8] {'dp','fsdp'}, use_global_device_ids=true, to_apply=%region_4.5 | all-reduce | flops 2 | bytes 16 | tf_op jit(solution)/shard_map/psum | solution.py:89
  110.7 125.1 %all-reduce.4.cloned.1.call-done = f32[64,512]{1,0:T(8,128)} async-done(((f32[64,512]{1,0:T(8,128)}), f32[64,512]{1,0:T(8,128)}) %all-reduce.4.cloned.1.call-update) | async-done | bytes 131088 | tf_op jit(solution)/shard_map/psum | solution.py:89
  235.8 2.2 multiply_add_fusion
  238.0 33.7 %all-reduce.6.cloned.1.call-done = f32[512,64]{0,1:T(8,128)} async-done(((f32[512,64]{0,1:T(8,128)}), f32[512,64]{0,1:T(8,128)}) %all-reduce.6.cloned.1.call-update) | async-done | bytes 131088 | tf_op jit(solution)/shard_map/psum | solution.py:81
  271.7 2.2 multiply_add_fusion.1
  (29 shorter events, 0.4 us)
Async XLA Ops:
  7.2 15.8 %copy-start = (bf16[256,4096]{1,0:T(8,128)(2,1)S(1)}, bf16[256,4096]{1,0:T(8,128)(2,1)}, u32[]{:S(2)}) copy-start(bf16[256,4096]{1,0:T(8,128)(2,1)} %param.10) | copy-start | bytes 6291460
  7.2 4.3 %copy-start.3 = (f32[512,64]{0,1:T(8,128)S(1)}, f32[512,64]{0,1:T(8,128)}, u32[]{:S(2)}) copy-start(f32[512,64]{0,1:T(8,128)} %param.16) | copy-start | bytes 393220
  7.2 42.0 %all-gather.2.cloned.1.call-start = ((), (), s32[]{:S(2)}) async-start(), calls=%async_computation.1 | async-start | bytes 4718592 | tf_op jit(solution)/shard_map/all_gather | solution.py:36
  7.9 102.8 %reduce-scatter.2.cloned.1.call-start = ((), (), s32[]{:S(2)}) async-start(), calls=%async_computation.3 | async-start | bytes 1179648 | tf_op jit(solution)/shard_map/reduce_scatter | solution.py:88
  28.0 24.6 %copy-start.1 = (f32[64,512]{1,0:T(8,128)S(1)}, f32[64,512]{1,0:T(8,128)}, u32[]{:S(2)}) copy-start(f32[64,512]{1,0:T(8,128)} %param.17) | copy-start | bytes 393220
  28.0 24.6 %copy-start.5 = (bf16[256,64]{0,1:T(8,128)(2,1)S(1)}, bf16[256,64]{0,1:T(8,128)(2,1)}, u32[]{:S(2)}) copy-start(bf16[256,64]{0,1:T(8,128)(2,1)} %convolution_convert_fusion.1) | copy-start | bytes 98308
  56.4 3.0 %copy-start.2 = (bf16[256,2048]{1,0:T(8,128)(2,1)S(1)}, bf16[256,2048]{1,0:T(8,128)(2,1)}, u32[]{:S(2)}) copy-start(bf16[256,2048]{1,0:T(8,128)(2,1)} %param.13) | copy-start | bytes 3145732
  67.0 2.0 copy-start.6
  67.0 168.8 %copy-start.7 = (f32[64,512]{1,0:T(8,128)S(1)}, f32[64,512]{1,0:T(8,128)}, u32[]{:S(2)}) copy-start(f32[64,512]{1,0:T(8,128)} %param.19) | copy-start | bytes 393220
  67.0 204.7 %copy-start.4 = (f32[512,64]{0,1:T(8,128)S(1)}, f32[512,64]{0,1:T(8,128)}, u32[]{:S(2)}) copy-start(f32[512,64]{0,1:T(8,128)} %param.16) | copy-start | bytes 393220
  67.0 204.7 %copy-start.8 = (f32[512,64]{0,1:T(8,128)S(1)}, f32[512,64]{0,1:T(8,128)}, u32[]{:S(2)}) copy-start(f32[512,64]{0,1:T(8,128)} %param.18) | copy-start | bytes 393220
  68.9 166.9 %all-reduce.4.cloned.1.call-start = ((), (), s32[]{:S(2)}) async-start(), calls=%async_computation.2 | async-start | bytes 262144 | tf_op jit(solution)/shard_map/psum | solution.py:89
  69.8 201.8 %all-reduce.6.cloned.1.call-start = ((), (), s32[]{:S(2)}) async-start(), calls=%async_computation.4 | async-start | bytes 262144 | tf_op jit(solution)/shard_map/psum | solution.py:81
Sparse Core Ops, SparseCore 0:
  9.9 39.2 all-gather.1
  69.0 35.9 reduce-scatter.1
  111.1 124.5 all-reduce.3
  237.9 33.6 all-reduce.5
where the time goes:
time: 282 us
  waiting for transfers between devices  181 us (64%)
  blocking collectives  50.9 us (18%)
  between operations  16.9 us (6%)
  matrix products  14.2 us (5%)
  other arithmetic  11.1 us (4%)
  local copies, waits for them, and re-layouts  7.48 us (3%)
    psum x1, waiting for transfers between devices, per_device(): lax.psum((adapter_scale * up_term, loss_local, count_local), ('dp', 'fsdp'))  125 us
    psum x1, blocking collectives, per_device(): lax.psum((adapter_scale * up_term, loss_local, count_local), ('dp', 'fsdp'))  39.5 us
    psum x1, waiting for transfers between devices, per_device(): lax.psum(adapter_scale * lax.dot_general(columns, latent_grad, (((0,), (0...  33.7 us
    all_gather x1, waiting for transfers between devices, per_device(): lax.all_gather(value_weight_frozen, 'fsdp', axis=0, tiled=True)  21.2 us
    all_gather x1, blocking collectives, per_device(): lax.all_gather(down_factor_slice, 'fsdp', axis=0, tiled=True)  11.3 us
  transfers between devices with their start and end apart: 4, of which 3 were waited for; matrix products, arithmetic and copies ran while one was open for 4% of the time, Pallas kernels for 0%

commit v1 on v0

--- a/solution.py
+++ b/solution.py
@@ -78,12 +78,15 @@
     )
     count_local = seq_length.astype(jnp.float32)
     columns = hidden
-    down_map_gradient = lax.psum(
-        adapter_scale
-        * lax.dot_general(
-            columns, latent_grad, (((0,), (0,)), ((), ())), preferred_element_type=jnp.float32
+    down_map_gradient = jnp.sum(
+        lax.all_gather(
+            adapter_scale
+            * lax.dot_general(
+                columns, latent_grad, (((0,), (0,)), ((), ())), preferred_element_type=jnp.float32
+            ),
+            "dp",
         ),
-        "dp",
+        axis=0,
     )
     down_map_gradient = lax.psum_scatter(down_map_gradient, "fsdp", scatter_dimension=0, tiled=True)
     up_map_gradient, loss_sum, token_grand_count = lax.psum(

time: 282 us -> 327 us (1.16)
  waiting for transfers between devices: 181 us -> 215 us
  local copies, waits for them, and re-layouts: 7.48 us -> 13.5 us
  other arithmetic: 11.1 us -> 17 us
    all_gather x0 -> x1, waiting for transfers between devices: none -> 79.9 us  [per_device(): lax.all_gather(adapter_scale * lax.dot_general(columns, latent_grad, (((0...]
    psum x1, waiting for transfers between devices: 125 us -> 77 us  [per_device(): lax.psum((adapter_scale * up_term, loss_local, count_local), ('dp', 'fsdp'))]
    reduce_scatter x1, waiting for transfers between devices: 0.02 us -> 35.8 us  [per_device(): lax.psum_scatter(down_map_gradient, 'fsdp', scatter_dimension=0, tiled=True)]
    psum x1 -> x0, waiting for transfers between devices: 33.7 us -> none  [per_device(): lax.psum(adapter_scale * lax.dot_general(columns, latent_grad, (((0,), (0...]
    all_gather x0 -> x1, local copies, waits for them, and re-layouts: none -> 6.05 us  [per_device(): lax.all_gather(adapter_scale * lax.dot_general(columns, latent_grad, (((0...]
    reduce_sum x0 -> x1, other arithmetic: none -> 5.88 us  [per_device(): jnp.sum(lax.all_gather(adapter_scale * lax.dot_general(columns, latent_gr...]
  transfers between devices with their start and end apart: 4 -> 4, of which waited for: 3 -> 4; matrix products, arithmetic and copies ran while one was open for 4% -> 7% of each run, Pallas kernels for 0% -> 0%
where the time goes in v1:
time: 327 us
  waiting for transfers between devices  215 us (66%)
  blocking collectives  50.3 us (15%)
  other arithmetic  17 us (5%)
  between operations  16.9 us (5%)
  matrix products  14.2 us (4%)
  local copies, waits for them, and re-layouts  13.5 us (4%)
    all_gather x1, waiting for transfers between devices, per_device(): lax.all_gather(adapter_scale * lax.dot_general(columns, latent_grad, (((0...  79.9 us
    psum x1, waiting for transfers between devices, per_device(): lax.psum((adapter_scale * up_term, loss_local, count_local), ('dp', 'fsdp'))  77 us
    psum x1, blocking collectives, per_device(): lax.psum((adapter_scale * up_term, loss_local, count_local), ('dp', 'fsdp'))  38.9 us
    reduce_scatter x1, waiting for transfers between devices, per_device(): lax.psum_scatter(down_map_gradient, 'fsdp', scatter_dimension=0, tiled=True)  35.8 us
    all_gather x1, waiting for transfers between devices, per_device(): lax.all_gather(value_weight_frozen, 'fsdp', axis=0, tiled=True)  21.2 us
    all_gather x1, blocking collectives, per_device(): lax.all_gather(down_factor_slice, 'fsdp', axis=0, tiled=True)  11.3 us
  transfers between devices with their start and end apart: 4, of which 4 were waited for; matrix products, arithmetic and copies ran while one was open for 7% of the time, Pallas kernels for 0%

profile of v1, /device:TPU:0, one launch (start us, length us, event | category | flops | bytes accessed | tf_op | source)
XLA Modules:
  0.0 326.8 jit_solution(15288402735363591970)
XLA Ops:
  8.6 1.8 reshape.40
  10.4 1.0 reshape.39
  11.5 11.3 %all_gather.13 = bf16[4096,64]{0,1:T(8,128)(2,1)S(1)} all-gather(bf16[512,64]{0,1:T(8,128)(2,1)S(1)} %convert_element_type.36), channel_id=1, replica_groups=mesh['dp'=4,'fsdp'=8] {'fsdp'}, dimensions={0}, use_global_device_ids=true | all-gather | bytes 589824 | tf_op jit(solution)/shard_map/all_gather | solution.py:41
  22.9 1.4 convolution_convert_fusion.1
  24.3 0.7 fusion.10
  25.0 1.2 fusion.19
  26.3 1.8 divide_convert_fusion
  28.0 21.2 %all-gather.4.cloned.1.call-done = bf16[4096,512]{1,0:T(8,128)(2,1)} async-done(((bf16[512,512]{1,0:T(8,128)(2,1)}), bf16[4096,512]{1,0:T(8,128)(2,1)}) %all-gather.4.cloned.1.call-update) | async-done | bytes 4194320 | tf_op jit(solution)/shard_map/all_gather | solution.py:36
  49.2 3.4 %fusion.20 = f32[256,512]{1,0:T(8,128)S(1)} fusion(bf16[256,4096]{1,0:T(8,128)(2,1)S(1)} %copy-done, bf16[4096,512]{1,0:T(8,128)(2,1)} %all-gather.4.cloned.1.call-done), kind=kOutput, calls=%fused_computation.36 | convolution fusion | flops 1073741824 | bytes 6815744 | tf_op jit(solution)/shard_map/dot_general | solution.py:34
  53.1 3.3 %fusion.21 = f32[4,128,4,256]{3,1,2,0:T(8,128)} fusion(bf16[256,4,128,1]{0,2,3,1:T(8,128)(2,1)S(1)} %bitcast.53, bf16[4,4,256,256]{2,3,1,0:T(8,128)(2,1)} %divide_convert_fusion), kind=kOutput, calls=%fused_computation.37 | convolution fusion | flops 268435456 | bytes 4456448 | tf_op jit(solution)/shard_map/kgts,skd->tkgd/dot_general | solution.py:62
  56.4 3.0 copy.19
  59.5 3.6 %multiply_reduce_fusion = (f32[]{:T(128)}, bf16[256,2048]{1,0:T(8,128)(2,1)}) fusion(f32[256,2048]{1,0:T(8,128)} %copy.19, bf16[256,2048]{1,0:T(8,128)(2,1)S(1)} %copy-done.2, pred[256]{0:T(512)(128)(4,1)S(1)} %iota_compare_fusion.1), kind=kLoop, calls=%fused_computation.7 | loop fusion | flops 3145727 | bytes 4194564 | tf_op jit(solution)/shard_map/reduce_sum | solution.py:67
  63.1 1.5 copy.30
  64.6 2.4 fusion.9
  67.0 1.8 fusion.1
  68.9 0.9 convolution_multiply_fusion.2
  69.9 79.9 %all-gather.6.cloned.1.call-done = f32[16384,64]{0,1:T(8,128)} async-done(((f32[4096,64]{0,1:T(8,128)}), f32[16384,64]{0,1:T(8,128)}) %all-gather.6.cloned.1.call-update) | async-done | bytes 4194320 | tf_op jit(solution)/shard_map/all_gather | solution.py:82
  149.7 6.0 %reshape.43 = f32[4,4096,64]{1,0,2:T(4,128)} reshape(f32[16384,64]{0,1:T(8,128)} %all-gather.6.cloned.1.call-done) | data formatting | bytes 8388608 | tf_op jit(solution)/shard_map/all_gather | solution.py:82
  155.8 5.9 %reduce_sum.28 = f32[4096,64]{0,1:T(8,128)} reduce(f32[4,4096,64]{1,0,2:T(4,128)} %reshape.43, f32[]{:T(128)} %constant.11.clone.1), dimensions={0}, to_apply=%region_2.3 | reduce | flops 786432 | bytes 5242884 | tf_op jit(solution)/shard_map/reduce_sum | solution.py:81
  161.7 38.9 %all-reduce = (f32[]{:T(128)}, f32[]{:T(128)}) all-reduce(f32[]{:T(128)S(6)} %convert_element_type.47, f32[]{:T(128)} %get-tuple-element.11), channel_id=1, replica_groups=mesh['dp'=4,'fsdp'=8] {'dp','fsdp'}, use_global_device_ids=true, to_apply=%region_4.5 | all-reduce | flops 2 | bytes 16 | tf_op jit(solution)/shard_map/psum | solution.py:92
  201.9 77.0 %all-reduce.3.cloned.1.call-done = f32[64,512]{1,0:T(8,128)} async-done(((f32[64,512]{1,0:T(8,128)}), f32[64,512]{1,0:T(8,128)}) %all-reduce.3.cloned.1.call-update) | async-done | bytes 131088 | tf_op jit(solution)/shard_map/psum | solution.py:92
  278.9 2.2 multiply_add_fusion
  281.1 35.8 %reduce-scatter.2.cloned.1.call-done = f32[512,64]{0,1:T(8,128)} async-done(((f32[4096,64]{0,1:T(8,128)}), f32[512,64]{0,1:T(8,128)}) %reduce-scatter.2.cloned.1.call-update) | async-done | bytes 131088 | tf_op jit(solution)/shard_map/reduce_scatter | solution.py:91
  316.9 2.2 multiply_add_fusion.1
  (31 shorter events, 1.4 us)
Async XLA Ops:
  7.2 15.8 %copy-start = (bf16[256,4096]{1,0:T(8,128)(2,1)S(1)}, bf16[256,4096]{1,0:T(8,128)(2,1)}, u32[]{:S(2)}) copy-start(bf16[256,4096]{1,0:T(8,128)(2,1)} %param.10) | copy-start | bytes 6291460
  7.2 4.3 %copy-start.3 = (f32[512,64]{0,1:T(8,128)S(1)}, f32[512,64]{0,1:T(8,128)}, u32[]{:S(2)}) copy-start(f32[512,64]{0,1:T(8,128)} %param.16) | copy-start | bytes 393220
  7.2 42.0 %all-gather.4.cloned.1.call-start = ((), (), s32[]{:S(2)}) async-start(), calls=%async_computation.1 | async-start | bytes 4718592 | tf_op jit(solution)/shard_map/all_gather | solution.py:36
  7.9 141.8 %all-gather.6.cloned.1.call-start = ((), (), s32[]{:S(2)}) async-start(), calls=%async_computation.4 | async-start | bytes 5242880 | tf_op jit(solution)/shard_map/all_gather | solution.py:82
  28.0 24.6 %copy-start.1 = (f32[64,512]{1,0:T(8,128)S(1)}, f32[64,512]{1,0:T(8,128)}, u32[]{:S(2)}) copy-start(f32[64,512]{1,0:T(8,128)} %param.17) | copy-start | bytes 393220
  28.0 24.6 %copy-start.5 = (bf16[256,64]{0,1:T(8,128)(2,1)S(1)}, bf16[256,64]{0,1:T(8,128)(2,1)}, u32[]{:S(2)}) copy-start(bf16[256,64]{0,1:T(8,128)(2,1)} %convolution_convert_fusion.1) | copy-start | bytes 98308
  56.4 3.0 copy-start.2
  67.0 1.9 copy-start.6
  68.9 210.0 %all-reduce.3.cloned.1.call-start = ((), (), s32[]{:S(2)}) async-start(), calls=%async_computation.3 | async-start | bytes 262144 | tf_op jit(solution)/shard_map/psum | solution.py:92
  69.8 247.1 %reduce-scatter.2.cloned.1.call-start = ((), (), s32[]{:S(2)}) async-start(), calls=%async_computation.2 | async-start | bytes 1179648 | tf_op jit(solution)/shard_map/reduce_scatter | solution.py:91
  155.8 123.1 %copy-start.7 = (f32[64,512]{1,0:T(8,128)S(1)}, f32[64,512]{1,0:T(8,128)}, u32[]{:S(2)}) copy-start(f32[64,512]{1,0:T(8,128)} %param.19) | copy-start | bytes 393220
  155.8 161.1 %copy-start.4 = (f32[512,64]{0,1:T(8,128)S(1)}, f32[512,64]{0,1:T(8,128)}, u32[]{:S(2)}) copy-start(f32[512,64]{0,1:T(8,128)} %param.16) | copy-start | bytes 393220
  155.8 161.1 %copy-start.8 = (f32[512,64]{0,1:T(8,128)S(1)}, f32[512,64]{0,1:T(8,128)}, u32[]{:S(2)}) copy-start(f32[512,64]{0,1:T(8,128)} %param.18) | copy-start | bytes 393220
Sparse Core Ops, SparseCore 0:
  9.9 39.2 all-gather.3
  69.0 80.7 all-gather.5
  155.9 122.9 all-reduce.2
  281.9 34.9 reduce-scatter.1
